TPU v7x, 256 devices: a whole 4x4x8 slice. The times are simulated.
256 devices in a mesh: dp: 32 (over y, z_lo, x), tensor: 8 (over z_hi, core).
Axes of the slice: x: 4, y: 4, z: 8 (z_hi: 4, z_lo: 2; z = z_hi * 2 + z_lo), core: 2. Of those that a mesh axis runs over, the one named last changes fastest.
Arguments:
- hidden: bfloat16 [32768, 7168], P('dp', 'tensor'), parts along dimension 0, may hold values from -6 to 6
- w_dq: bfloat16 [7168, 1536], P('tensor'), may hold values from -0.0625 to 0.0625
- w_dkv: bfloat16 [7168, 576], P('tensor'), may hold values from -0.0625 to 0.0625
- q_gain: float32 [1536], replicated, may hold values from 0.1 to 1.9
- kv_gain: float32 [512], replicated, may hold values from 0.1 to 1.9
- w_uq: bfloat16 [1536, 12288], P(None, 'tensor'), may hold values from -0.15625 to 0.15625
- w_ukv: bfloat16 [512, 16384], P(None, 'tensor'), may hold values from -0.25 to 0.25
Outputs:
- queries: bfloat16 [32768, 12288], P('dp', 'tensor'), parts along dimension 0
- keys_values: bfloat16 [32768, 16384], P('dp', 'tensor'), parts along dimension 0
- rotary_key: bfloat16 [32768, 64], P(('dp', 'tensor')), parts along dimension 0
There are 32 independent parts, one for each index of `dp`. A program takes and returns all parts, laid end to end along the dimension named above; an argument that names none is the same for every part. Nothing has to cross between parts.
All inputs are finite; a program needn't handle non-finite values.
Results may differ from a plain program's by a relative error of at most 0.0049.
Values may be sent and summed in bfloat16 or wider, within the bound.
No kernel may reach another device: no remote copies, remote signals or barrier semaphores. Data moves between devices by JAX's collectives and lax.ppermute only.
A program may use at most 128 MiB of HBM per device.

v0:
```python
import jax
import jax.numpy as jnp
from jax import lax
from jax.sharding import PartitionSpec as P

NOPE = 128
ROPE = 64


def rotate(values, angle):
    half = values.shape[-1] // 2
    first = values[..., :half]
    second = values[..., half:]
    cosine = jnp.cos(angle)
    sine = jnp.sin(angle)
    return jnp.concatenate(
        [first * cosine - second * sine, second * cosine + first * sine], axis=-1
    )


def angles(first_row, count, half):
    positions = (first_row + lax.iota(jnp.int32, count)).astype(jnp.float32)
    freqs = 50000.0 ** (-jnp.arange(half, dtype=jnp.float32) / half)
    return positions[:, None] * freqs[None, :]


def normalize(block, gain):
    scale = lax.rsqrt(jnp.mean(block * block, axis=1, keepdims=True) + 1e-06)
    return (block * scale * gain[None, :]).astype(jnp.bfloat16)


def shards(hidden, w_dq, w_dkv, q_gain, kv_gain, w_uq, w_ukv):
    q_width = w_dq.shape[1]
    kv_width = kv_gain.shape[0]
    rope_width = w_dkv.shape[1] - kv_width
    head_width = NOPE + ROPE
    local_heads = w_uq.shape[1] // head_width
    total_rows = hidden.shape[0]
    share = total_rows // lax.axis_size("tensor")
    own_start = lax.axis_index("tensor") * share
    down = lax.psum_scatter(
        jnp.concatenate(
            [
                jnp.dot(hidden, w_dq, preferred_element_type=jnp.float32),
                jnp.dot(hidden, w_dkv, preferred_element_type=jnp.float32),
            ],
            axis=1,
        ),
        "tensor",
        scatter_dimension=0,
        tiled=True,
    )
    latent = jnp.concatenate(
        [
            normalize(down[:, :q_width], q_gain),
            normalize(down[:, q_width : q_width + kv_width], kv_gain),
        ],
        axis=1,
    )
    piece = lax.all_gather(latent, "tensor", axis=0, tiled=True)
    count = piece.shape[0]
    query_full = jnp.dot(piece[:, :q_width], w_uq, preferred_element_type=jnp.float32)
    query_full = query_full.reshape(count, local_heads, head_width)
    angle = angles(jnp.int32(0), count, ROPE // 2)
    turned = rotate(query_full[:, :, NOPE:], angle[:, None, :])
    query_out = jnp.concatenate([query_full[:, :, :NOPE], turned], axis=2)
    query_out = query_out.reshape(count, local_heads * head_width).astype(jnp.bfloat16)
    kv_out = jnp.dot(piece[:, q_width:], w_ukv, preferred_element_type=jnp.float32).astype(
        jnp.bfloat16
    )
    both = jnp.concatenate([query_out, kv_out], axis=1)
    mine = down[:, q_width + kv_width :]
    rotary_key = rotate(mine, angles(own_start, share, rope_width // 2)).astype(jnp.bfloat16)
    query_cols = local_heads * head_width
    return (both[:, :query_cols], both[:, query_cols:], rotary_key)


def solution(mesh):
    in_specs = (
        P("dp", "tensor"),
        P("tensor", None),
        P("tensor", None),
        P(),
        P(),
        P(None, "tensor"),
        P(None, "tensor"),
    )
    out_specs = (P("dp", "tensor"), P("dp", "tensor"), P(("dp", "tensor"), None))
    return jax.shard_map(shards, mesh=mesh, in_specs=in_specs, out_specs=out_specs, check_vma=False)
```

profile of v0, /device:TPU:1, one launch (start us, length us, event | category | flops | bytes accessed | tf_op | source)
XLA Modules:
  0.0 218.4 jit_solution(12857306435849263300)
XLA Ops:
  7.2 0.0 copy-start
  7.2 0.0 reduce-scatter.2.cloned.1.call-start
  7.2 1.7 copy-done
  8.9 0.0 copy-start.3
  9.0 0.0 copy-start.4
  9.0 5.2 %fusion.11 = f32[1024,1536]{0,1:T(8,128)S(1)} fusion(bf16[1024,896]{1,0:T(8,128)(2,1)} %param.7, bf16[896,1536]{1,0:T(8,128)(2,1)S(1)} %copy-done), kind=kOutput, calls=%fused_computation.32 | convolution fusion | flops 2818572288 | bytes 10878976 | tf_op jit(solution)/shard_map/dot_general | solution.py:44
  14.2 0.0 copy-done.3
  14.2 0.0 copy-done.4
  14.2 2.8 %fusion.12 = f32[1024,576]{0,1:T(8,128)} fusion(bf16[1024,896]{1,0:T(8,128)(2,1)S(1)} %copy-done.3, bf16[896,576]{0,1:T(8,128)(2,1)S(1)} %copy-done.4), kind=kOutput, calls=%fused_computation.33 | convolution fusion | flops 1056964608 | bytes 5226496 | tf_op jit(solution)/shard_map/dot_general | solution.py:45
  17.0 6.4 %pad_maximum_fusion = f32[1024,2112]{0,1:T(8,128)} fusion(f32[1024,576]{0,1:T(8,128)} %fusion.12, f32[1024,1536]{0,1:T(8,128)S(1)} %fusion.11), kind=kLoop, calls=%fused_computation | loop fusion | flops 2162688 | bytes 17301504 | tf_op jit(solution)/shard_map/concatenate | solution.py:42
  23.4 0.0 copy-start.1
  23.4 0.0 reduce-scatter.2.cloned.1.call-update
  23.4 0.2 all-gather.2.cloned.1.call-start
  23.7 101.5 %reduce-scatter.2.cloned.1.call-done = f32[128,2112]{0,1:T(8,128)} async-done(((f32[1024,2112]{0,1:T(8,128)}), f32[128,2112]{0,1:T(8,128)}) %reduce-scatter.2.cloned.1.call-update) | async-done | bytes 1081360 | tf_op jit(solution)/shard_map/reduce_scatter | solution.py:41
  125.2 1.3 multiply_reduce_fusion
  126.5 1.0 multiply_reduce_fusion.1
  127.6 0.0 copy-done.1
  127.6 1.4 multiply_convert_fusion
  129.0 0.0 copy-done.2
  129.0 1.1 multiply_convert_fusion.1
  130.1 0.8 pad_maximum_fusion.2
  130.9 0.0 all-gather.2.cloned.1.call-update
  131.0 0.5 multiply_cosine_fusion
  131.5 0.9 fusion.8
  132.4 0.6 pad_maximum_fusion.3
  133.0 57.0 %all-gather.2.cloned.1.call-done = bf16[1024,2048]{0,1:T(8,128)(2,1)} async-done(((bf16[128,2048]{0,1:T(8,128)(2,1)}), bf16[1024,2048]{0,1:T(8,128)(2,1)}) %all-gather.2.cloned.1.call-update) | async-done | bytes 4194320 | tf_op jit(solution)/shard_map/all_gather | solution.py:60
  190.0 8.1 %fusion = f32[1024,1536]{0,1:T(8,128)S(1)} fusion(bf16[1536,1536]{1,0:T(8,128)(2,1)} %param.12, bf16[1024,2048]{0,1:T(8,128)(2,1)} %all-gather.2.cloned.1.call-done), kind=kOutput, calls=%fused_computation.3 | convolution fusion | flops 4831838208 | bytes 14155776 | tf_op jit(solution)/shard_map/dot_general | solution.py:62
  198.1 0.3 slice.69
  198.5 0.3 subtract_convert_fusion
  198.8 1.9 pad_maximum_fusion.1
  200.7 4.6 %copy.18 = bf16[1024,1536]{1,0:T(8,128)(2,1)} copy(bf16[1024,1536]{0,1:T(8,128)(2,1)} %bitcast.8) | data formatting | bytes 6291456
  205.3 6.3 %convolution_convert_fusion = bf16[1024,2048]{1,0:T(8,128)(2,1)} fusion(bf16[512,2048]{1,0:T(8,128)(2,1)} %param.13, bf16[1024,2048]{0,1:T(8,128)(2,1)} %all-gather.2.cloned.1.call-done), kind=kOutput, calls=%fused_computation.2 | convolution fusion | flops 2149580800 | bytes 7340032 | tf_op jit(solution)/shard_map/dot_general | solution.py:68
  (6 shorter events, 0.0 us)
Async XLA Ops:
  7.2 1.8 copy-start
  7.2 118.0 %reduce-scatter.2.cloned.1.call-start = ((), (), s32[]{:S(2)}) async-start(), calls=%async_computation.1 | async-start | bytes 9732096 | tf_op jit(solution)/shard_map/reduce_scatter | solution.py:41
  8.9 5.2 %copy-start.3 = (bf16[1024,896]{1,0:T(8,128)(2,1)S(1)}, bf16[1024,896]{1,0:T(8,128)(2,1)}, u32[]{:S(2)}) copy-start(bf16[1024,896]{1,0:T(8,128)(2,1)} %param.7) | copy-start | bytes 5505028
  9.0 5.2 %copy-start.4 = (bf16[896,576]{0,1:T(8,128)(2,1)S(1)}, bf16[896,576]{0,1:T(8,128)(2,1)}, u32[]{:S(2)}) copy-start(bf16[896,576]{0,1:T(8,128)(2,1)} %param.9) | copy-start | bytes 3096580
  23.4 104.2 %copy-start.1 = (f32[1536]{0:T(1024)S(1)}, f32[1536]{0:T(1024)}, u32[]{:S(2)}) copy-start(f32[1536]{0:T(1024)} %param.10) | copy-start | bytes 18436
  23.4 105.6 %copy-start.2 = (f32[512]{0:T(512)S(1)}, f32[512]{0:T(512)}, u32[]{:S(2)}) copy-start(f32[512]{0:T(512)} %param.11) | copy-start | bytes 6148
  23.4 166.5 %all-gather.2.cloned.1.call-start = ((), (), s32[]{:S(2)}) async-start(), calls=%async_computation.2 | async-start | bytes 4718592 | tf_op jit(solution)/shard_map/all_gather | solution.py:60
Sparse Core Ops, SparseCore 0:
  23.6 101.5 reduce-scatter.1
  131.0 58.8 all-gather.1
where the time goes:
time: 219 us; the launch traced here: 218 us
  waiting for transfers between devices  158 us (72%)
  matrix products  22.5 us (10%)
  other arithmetic  16.4 us (7%)
  between operations  14.1 us (6%)
  local copies, waits for them, and re-layouts  6.69 us (3%)
    reduce_scatter x1, waiting for transfers between devices, shards(): lax.psum_scatter(jnp.concatenate([jnp.dot(hidden, w_dq, preferred_element...  101 us
    all_gather x1, waiting for transfers between devices, shards(): piece = lax.all_gather(latent, 'tensor', axis=0, tiled=True)  57 us
    dot_general x1, matrix products, shards(): jnp.dot(piece[:, :q_width], w_uq, preferred_element_type=jnp.float32)  8.14 us
    concatenate x1, other arithmetic, shards(): jnp.concatenate([jnp.dot(hidden, w_dq, preferred_element_type=jnp.float32...  6.4 us
    unnamed x11, local copies, waits for them, and re-layouts  6.37 us
    dot_general x1, matrix products, shards(): jnp.dot(piece[:, q_width:], w_ukv, preferred_element_type=jnp.float32)  6.32 us
    dot_general x1, matrix products, shards(): jnp.dot(hidden, w_dq, preferred_element_type=jnp.float32)  5.2 us
  transfers between devices with their start and end apart: 2, of which 2 were waited for; matrix products, arithmetic and copies ran while one was open for 1% of the time, Pallas kernels for 0%

commit v1 on v0

--- a/solution.py
+++ b/solution.py
@@ -57,7 +57,8 @@
         ],
         axis=1,
     )
-    piece = lax.all_gather(latent, "tensor", axis=0, tiled=True)
+    outgoing = jnp.stack([latent] * lax.axis_size("tensor"))
+    piece = jnp.concatenate(lax.all_to_all(outgoing, "tensor", 0, 0), axis=0)
     count = piece.shape[0]
     query_full = jnp.dot(piece[:, :q_width], w_uq, preferred_element_type=jnp.float32)
     query_full = query_full.reshape(count, local_heads, head_width)

time: 219 us -> 266 us (1.21)
  waiting for transfers between devices: 158 us -> 193 us
  starting transfers between devices: 0.26 us -> 9.23 us
  local copies, waits for them, and re-layouts: 6.69 us -> 10.5 us
    all_to_all x0 -> x1, waiting for transfers between devices: none -> 91.3 us  [shards(): piece = jnp.concatenate(lax.all_to_all(outgoing, 'tensor', 0, 0), axis=0)]
    all_gather x1 -> x0, waiting for transfers between devices: 57 us -> none  [shards(): piece = lax.all_gather(latent, 'tensor', axis=0, tiled=True)]
    all_to_all x0 -> x1, starting transfers between devices: none -> 9.19 us  [shards(): piece = jnp.concatenate(lax.all_to_all(outgoing, 'tensor', 0, 0), axis=0)]
where the time goes in v1:
time: 266 us
  waiting for transfers between devices  193 us (73%)
  matrix products  22.4 us (8%)
  other arithmetic  16.3 us (6%)
  between operations  14.1 us (5%)
  local copies, waits for them, and re-layouts  10.5 us (4%)
  starting transfers between devices  9.23 us (3%)
    reduce_scatter x1, waiting for transfers between devices, shards(): lax.psum_scatter(jnp.concatenate([jnp.dot(hidden, w_dq, preferred_element...  102 us
    all_to_all x1, waiting for transfers between devices, shards(): piece = jnp.concatenate(lax.all_to_all(outgoing, 'tensor', 0, 0), axis=0)  91.3 us
    all_to_all x1, starting transfers between devices, shards(): piece = jnp.concatenate(lax.all_to_all(outgoing, 'tensor', 0, 0), axis=0)  9.19 us
    dot_general x1, matrix products, shards(): jnp.dot(piece[:, :q_width], w_uq, preferred_element_type=jnp.float32)  8.12 us
    concatenate x1, other arithmetic, shards(): jnp.concatenate([jnp.dot(hidden, w_dq, preferred_element_type=jnp.float32...  6.39 us
    unnamed x11, local copies, waits for them, and re-layouts  6.37 us
    dot_general x1, matrix products, shards(): jnp.dot(piece[:, q_width:], w_ukv, preferred_element_type=jnp.float32)  6.28 us
  transfers between devices with their start and end apart: 2, of which 2 were waited for; matrix products, arithmetic and copies ran while one was open for 1% of the time, Pallas kernels for 0%

profile of v1, /device:TPU:1, one launch (start us, length us, event | category | flops | bytes accessed | tf_op | source)
XLA Modules:
  0.0 265.7 jit_solution(4853611331293507995)
XLA Ops:
  7.2 0.0 copy-start
  7.2 0.0 reduce-scatter.2.cloned.1.call-start
  7.2 1.7 copy-done
  8.9 0.0 copy-start.3
  9.0 0.0 copy-start.4
  9.0 5.2 %fusion.11 = f32[1024,1536]{0,1:T(8,128)S(1)} fusion(bf16[1024,896]{1,0:T(8,128)(2,1)} %param.7, bf16[896,1536]{1,0:T(8,128)(2,1)S(1)} %copy-done), kind=kOutput, calls=%fused_computation.32 | convolution fusion | flops 2818572288 | bytes 10878976 | tf_op jit(solution)/shard_map/dot_general | solution.py:44
  14.2 0.0 copy-done.3
  14.2 0.0 copy-done.4
  14.2 2.8 %fusion.12 = f32[1024,576]{0,1:T(8,128)} fusion(bf16[1024,896]{1,0:T(8,128)(2,1)S(1)} %copy-done.3, bf16[896,576]{0,1:T(8,128)(2,1)S(1)} %copy-done.4), kind=kOutput, calls=%fused_computation.33 | convolution fusion | flops 1056964608 | bytes 5226496 | tf_op jit(solution)/shard_map/dot_general | solution.py:45
  17.0 6.4 %pad_maximum_fusion = f32[1024,2112]{0,1:T(8,128)} fusion(f32[1024,576]{0,1:T(8,128)} %fusion.12, f32[1024,1536]{0,1:T(8,128)S(1)} %fusion.11), kind=kLoop, calls=%fused_computation | loop fusion | flops 2162688 | bytes 17301504 | tf_op jit(solution)/shard_map/concatenate | solution.py:42
  23.4 0.0 reduce-scatter.2.cloned.1.call-update
  23.4 101.7 %reduce-scatter.2.cloned.1.call-done = f32[128,2112]{0,1:T(8,128)} async-done(((f32[1024,2112]{0,1:T(8,128)}), f32[128,2112]{0,1:T(8,128)}) %reduce-scatter.2.cloned.1.call-update) | async-done | bytes 1081360 | tf_op jit(solution)/shard_map/reduce_scatter | solution.py:41
  125.1 1.3 multiply_reduce_fusion
  126.5 1.0 multiply_reduce_fusion.1
  127.5 0.0 copy-done.1
  127.6 1.4 multiply_convert_fusion
  129.0 0.0 copy-done.2
  129.0 1.1 multiply_convert_fusion.1
  130.1 0.8 pad_maximum_fusion.2
  130.9 1.2 copy.17
  132.1 2.6 stack.2
  134.7 9.2 %all-to-all-start = ((bf16[8,128,2048]{2,1,0:T(8,128)(2,1)}), bf16[8,128,2048]{2,1,0:T(8,128)(2,1)}, u32[]{:S(2)}, u32[]{:S(2)}) async-start(bf16[8,128,2048]{2,1,0:T(8,128)(2,1)} %stack.2), calls=%async_computation.1 | async-start | bytes 8388608 | tf_op jit(solution)/shard_map/all_to_all | solution.py:61
  143.9 0.5 multiply_cosine_fusion
  144.5 0.9 fusion.8
  145.4 0.6 pad_maximum_fusion.3
  146.0 91.3 %all-to-all-done = bf16[8,128,2048]{2,1,0:T(8,128)(2,1)} async-done(((bf16[8,128,2048]{2,1,0:T(8,128)(2,1)}), bf16[8,128,2048]{2,1,0:T(8,128)(2,1)}, u32[]{:S(2)}, u32[]{:S(2)}) %all-to-all-start) | async-done | bytes 4194336 | tf_op jit(solution)/shard_map/all_to_all | solution.py:61
  237.3 8.1 %fusion = f32[1024,1536]{0,1:T(8,128)S(1)} fusion(bf16[1536,1536]{1,0:T(8,128)(2,1)} %param.12, bf16[1024,2048]{1,0:T(8,128)(2,1)} %bitcast), kind=kOutput, calls=%fused_computation.3 | convolution fusion | flops 4831838208 | bytes 14155776 | tf_op jit(solution)/shard_map/dot_general | solution.py:63
  245.4 0.3 slice.69
  245.7 0.3 subtract_convert_fusion
  246.1 1.9 pad_maximum_fusion.1
  247.9 4.6 %copy.19 = bf16[1024,1536]{1,0:T(8,128)(2,1)} copy(bf16[1024,1536]{0,1:T(8,128)(2,1)} %bitcast.9) | data formatting | bytes 6291456
  252.6 6.3 %convolution_convert_fusion = bf16[1024,2048]{1,0:T(8,128)(2,1)} fusion(bf16[512,2048]{1,0:T(8,128)(2,1)} %param.13, bf16[1024,2048]{1,0:T(8,128)(2,1)} %bitcast), kind=kOutput, calls=%fused_computation.2 | convolution fusion | flops 2149580800 | bytes 7340032 | tf_op jit(solution)/shard_map/dot_general | solution.py:69
  (7 shorter events, 0.0 us)
Async XLA Ops:
  7.2 1.8 copy-start
  7.2 118.0 %reduce-scatter.2.cloned.1.call-start = ((), (), s32[]{:S(2)}) async-start(), calls=%async_computation.2 | async-start | bytes 9732096 | tf_op jit(solution)/shard_map/reduce_scatter | solution.py:41
  8.9 5.2 %copy-start.3 = (bf16[1024,896]{1,0:T(8,128)(2,1)S(1)}, bf16[1024,896]{1,0:T(8,128)(2,1)}, u32[]{:S(2)}) copy-start(bf16[1024,896]{1,0:T(8,128)(2,1)} %param.7) | copy-start | bytes 5505028
  9.0 5.2 %copy-start.4 = (bf16[896,576]{0,1:T(8,128)(2,1)S(1)}, bf16[896,576]{0,1:T(8,128)(2,1)}, u32[]{:S(2)}) copy-start(bf16[896,576]{0,1:T(8,128)(2,1)} %param.9) | copy-start | bytes 3096580
  23.4 104.2 %copy-start.1 = (f32[1536]{0:T(1024)S(1)}, f32[1536]{0:T(1024)}, u32[]{:S(2)}) copy-start(f32[1536]{0:T(1024)} %param.10) | copy-start | bytes 18436
  23.4 105.6 %copy-start.2 = (f32[512]{0:T(512)S(1)}, f32[512]{0:T(512)}, u32[]{:S(2)}) copy-start(f32[512]{0:T(512)} %param.11) | copy-start | bytes 6148
  134.7 102.6 %all-to-all-start = ((bf16[8,128,2048]{2,1,0:T(8,128)(2,1)}), bf16[8,128,2048]{2,1,0:T(8,128)(2,1)}, u32[]{:S(2)}, u32[]{:S(2)}) async-start(bf16[8,128,2048]{2,1,0:T(8,128)(2,1)} %stack.2), calls=%async_computation.1 | async-start | bytes 8388608 | tf_op jit(solution)/shard_map/all_to_all | solution.py:61
Sparse Core Ops, SparseCore 0:
  23.5 101.5 reduce-scatter.1
